TPU v7x, 256 devices: a whole 4x4x8 slice. The times are simulated.
256 devices in a mesh: state: 256 (over y, z, x, core).
Axes of the slice: x: 4, y: 4, z: 8, core: 2. Of those that a mesh axis runs over, the one named last changes fastest.
Arguments:
- transitions: float32 [4096, 16, 4096], P('state'), may hold values from 0 to 1, as said below
- costs: float32 [4096, 16, 128], P('state'), may hold values from 0 to 4
- valid_counts: int32 [4096], P('state'), may hold values from 1 to 16
- start_values: float32 [4096, 128], P('state'), may hold values from -12 to 12
- ref_state: int32 [1], replicated, may hold values from 0 to 4095
Outputs:
- relative_values: float32 [4096, 128], P('state')
- lower_bounds: float32 [4, 128], replicated
- upper_bounds: float32 [4, 128], replicated
Inputs may be any that keep to these rules, and one draw needn't show every extreme that they name: Every entry is nonnegative and each row transitions[s, a, :] sums to one up to float32 rounding. Actions 0 to valid_counts[s] - 1 are allowed in state s.
All inputs are finite; a program needn't handle non-finite values.
Results may differ from a plain program's by a relative error of at most 0.00017.
Values sent between devices are 32-bit elements; how exact they have to be, the bound alone decides.
A program may use at most 64 MiB of HBM per device.

v0:
```python
import jax
import jax.numpy as jnp
from jax import lax
from jax.sharding import Mesh
from jax.sharding import PartitionSpec as P

ITERS = 4
STATE = ("state_0", "state_1", "state_2", "state_3")


big_value = 1e30


def over_axes(x, axes):
    for axis in axes:
        x = lax.pmax(x, axis)
    return x


def local(transitions, costs, valid_counts, start_values, ref_state):
    local_states = transitions.shape[0]
    actions = transitions.shape[1]
    scenarios = start_values.shape[1]
    flat_rows = transitions.reshape(local_states * actions, transitions.shape[2])
    allowed = jnp.arange(actions, dtype=jnp.int32)[None, :] < valid_counts[:, None]
    my_index = lax.axis_index(STATE)
    first_state = my_index * local_states
    owner_index = ref_state[0] // local_states
    offset = jnp.clip(ref_state[0] - first_state, 0, local_states - 1)
    is_owner = owner_index == my_index
    lower_list = []
    upper_list = []
    unshifted = start_values
    for iteration in range(ITERS):
        field_all = lax.all_gather(unshifted, STATE, axis=0, tiled=True)
        bellman_expected = jnp.dot(
            flat_rows,
            field_all,
            precision=lax.Precision.HIGHEST,
            preferred_element_type=jnp.float32,
        )
        q_values = costs + bellman_expected.reshape(local_states, actions, scenarios)
        q_values = jnp.where(allowed[:, :, None], q_values, jnp.float32(big_value))
        best_value = jnp.min(q_values, axis=1)
        increase = best_value - unshifted
        lower_list.append(jnp.min(increase, axis=0))
        upper_list.append(jnp.max(increase, axis=0))
        unshifted = best_value
    local_row = lax.dynamic_slice_in_dim(unshifted, offset, 1, 0)
    masked_row = jnp.where(is_owner, local_row, jnp.float32(-big_value))
    ref_row, upper_all, negated_all = (
        over_axes(masked_row, STATE),
        over_axes(jnp.stack(upper_list), STATE),
        over_axes(-jnp.stack(lower_list), STATE),
    )
    return (unshifted - ref_row, -negated_all, upper_all)


def solution(mesh):
    split = Mesh(mesh.devices.reshape(4, 8, 4, 2), ("state_0", "state_1", "state_2", "state_3"))
    return jax.shard_map(
        local,
        mesh=split,
        in_specs=(P(STATE, None, None), P(STATE, None, None), P(STATE), P(STATE, None), P()),
        out_specs=(P(STATE, None), P(), P()),
        check_vma=False,
    )
```

profile of v0, /device:TPU:1, one launch (start us, length us, event | category | flops | bytes accessed | tf_op | source)
XLA Modules:
  0.0 506.4 jit_solution(16758565774394789343)
XLA Ops:
  7.2 0.0 all-gather.5.cloned.1.call-start
  7.2 0.7 all-gather.5.cloned.1.call-update
  7.9 0.0 all-gather.7.cloned.1.call-start
  7.9 0.7 iota_compare_fusion
  8.7 111.4 %all-gather.5.cloned.1.call-done = f32[4096,128]{1,0:T(8,128)} async-done(((f32[16,128]{1,0:T(8,128)}), f32[4096,128]{1,0:T(8,128)}) %all-gather.5.cloned.1.call-update) | async-done | bytes 2097168 | tf_op jit(solution)/shard_map/all_gather | solution.py:35
  120.0 6.9 %fusion.8 = f32[16,128]{1,0:T(8,128)} fusion(f32[16,16,128]{2,1,0:T(8,128)} %param.6, f32[16,16,4096]{2,1,0:T(8,128)} %param.5, f32[4096,128]{1,0:T(8,128)} %all-gather.5.cloned.1.call-done, pred[16,16]{1,0:T(8,128)(4,1)S(1)} %iota_compare_fusion), kind=kOutput, calls=%fused_computation.7 | convolution fusion | flops 1610708992 | bytes 6430976 | tf_op jit(solution)/shard_map/dot_general | solution.py:36
  127.0 0.0 all-gather.7.cloned.1.call-update
  127.0 0.0 all-gather.9.cloned.1.call-start
  127.1 103.3 %all-gather.7.cloned.1.call-done = f32[4096,128]{1,0:T(8,128)} async-done(((f32[16,128]{1,0:T(8,128)}), f32[4096,128]{1,0:T(8,128)}) %all-gather.7.cloned.1.call-update) | async-done | bytes 2097168 | tf_op jit(solution)/shard_map/all_gather | solution.py:35
  230.3 6.3 %convolution_bitcast_fusion.2 = f32[256,128]{0,1:T(8,128)S(1)} fusion(f32[4096,128]{1,0:T(8,128)} %all-gather.7.cloned.1.call-done, f32[256,4096]{1,0:T(8,128)} %bitcast.44), kind=kOutput, calls=%fused_computation.6 | convolution fusion | flops 1610612736 | bytes 6422528 | tf_op jit(solution)/shard_map/dot_general | solution.py:36
  236.6 0.1 copy.8
  236.7 0.0 copy-done
  236.8 0.7 select_reduce_fusion.2
  237.5 0.0 all-gather.9.cloned.1.call-update
  237.5 0.2 all-gather.11.cloned.1.call-start
  237.7 103.1 %all-gather.9.cloned.1.call-done = f32[4096,128]{1,0:T(8,128)} async-done(((f32[16,128]{1,0:T(8,128)}), f32[4096,128]{1,0:T(8,128)}) %all-gather.9.cloned.1.call-update) | async-done | bytes 2097168 | tf_op jit(solution)/shard_map/all_gather | solution.py:35
  340.8 6.3 %convolution_bitcast_fusion.1 = f32[256,128]{0,1:T(8,128)S(1)} fusion(f32[4096,128]{1,0:T(8,128)} %all-gather.9.cloned.1.call-done, f32[256,4096]{1,0:T(8,128)} %bitcast.45), kind=kOutput, calls=%fused_computation.5 | convolution fusion | flops 1610612736 | bytes 6422528 | tf_op jit(solution)/shard_map/dot_general | solution.py:36
  347.1 0.1 copy.9
  347.2 0.7 select_reduce_fusion.1
  347.9 0.0 all-gather.11.cloned.1.call-update
  348.6 0.0 copy-start.1
  348.6 0.0 copy-start.4
  348.6 102.6 %all-gather.11.cloned.1.call-done = f32[4096,128]{1,0:T(8,128)} async-done(((f32[16,128]{1,0:T(8,128)}), f32[4096,128]{1,0:T(8,128)}) %all-gather.11.cloned.1.call-update) | async-done | bytes 2097168 | tf_op jit(solution)/shard_map/all_gather | solution.py:35
  451.2 6.3 %convolution_bitcast_fusion = f32[256,128]{0,1:T(8,128)S(1)} fusion(f32[4096,128]{1,0:T(8,128)} %all-gather.11.cloned.1.call-done, f32[256,4096]{1,0:T(8,128)} %bitcast.46), kind=kOutput, calls=%fused_computation.4 | convolution fusion | flops 1610612736 | bytes 6422528 | tf_op jit(solution)/shard_map/dot_general | solution.py:36
  457.5 0.1 copy.10
  457.6 0.1 select_reduce_fusion
  457.8 8.5 %all-reduce.2 = (f32[1,128]{1,0:T(1,128)S(1)}, f32[4,128]{1,0:T(4,128)S(1)}, f32[4,128]{1,0:T(4,128)S(1)}) all-reduce(f32[1,128]{1,0:T(1,128)S(1)} %broadcast_select_fusion, f32[4,128]{1,0:T(4,128)S(1)} %get-tuple-element.29, ...), channel_id=1, replica_groups=mesh['state_0'=4,'state_1'=8,'state_2'=4,'state_3'=2] {'state_0'}, use_global_device_ids=true, to_apply=%region_4.5 | all-reduce | flops 1152 | bytes 9216 | tf_op jit(solution)/shard_map/pmax | solution.py:16
  466.4 13.0 %all-reduce = (f32[1,128]{1,0:T(1,128)S(1)}, f32[4,128]{1,0:T(4,128)S(1)}, f32[4,128]{1,0:T(4,128)S(1)}) all-reduce(f32[1,128]{1,0:T(1,128)S(1)} %get-tuple-element.23, f32[4,128]{1,0:T(4,128)S(1)} %get-tuple-element.24, f32[4,128]{1,0:T(4,128)S(1)} %get-tuple-element.25), channel_id=1, replica_groups=mesh['state_0'=4,'state_1'=8,'state_2'=4,'state_3'=2] {'state_1'}, use_global_device_ids=true, to_apply=%region_5.6 | all-reduce | flops 1152 | bytes 9216 | tf_op jit(solution)/shard_map/pmax | solution.py:16
  479.4 8.5 %all-reduce.1 = (f32[1,128]{1,0:T(1,128)S(1)}, f32[4,128]{1,0:T(4,128)S(1)}, f32[4,128]{1,0:T(4,128)S(1)}) all-reduce(f32[1,128]{1,0:T(1,128)S(1)} %get-tuple-element.17, f32[4,128]{1,0:T(4,128)S(1)} %get-tuple-element.18, f32[4,128]{1,0:T(4,128)S(1)} %get-tuple-element.19), channel_id=1, replica_groups=mesh['state_0'=4,'state_1'=8,'state_2'=4,'state_3'=2] {'state_2'}, use_global_device_ids=true, to_apply=%region_6.7 | all-reduce | flops 1152 | bytes 9216 | tf_op jit(solution)/shard_map/pmax | solution.py:16
  487.9 10.8 %all-reduce.3 = (f32[128]{0:T(128)S(1)}, f32[4,128]{1,0:T(4,128)S(1)}, f32[4,128]{1,0:T(4,128)}) all-reduce(f32[128]{0:T(128)S(1)} %bitcast.55, f32[4,128]{1,0:T(4,128)S(1)} %get-tuple-element.21, f32[4,128]{1,0:T(4,128)S(1)} %get-tuple-element.22), channel_id=1, replica_groups=mesh['state_0'=4,'state_1'=8,'state_2'=4,'state_3'=2] {'state_3'}, use_global_device_ids=true, to_apply=%region_7.8 | all-reduce | flops 1152 | bytes 9216 | tf_op jit(solution)/shard_map/pmax | solution.py:16
  498.7 0.6 broadcast_subtract_fusion
  499.3 0.6 neg.7
  (10 shorter events, 0.1 us)
Async XLA Ops:
  7.2 112.9 %all-gather.5.cloned.1.call-start = ((), (), s32[]{:S(2)}) async-start(), calls=%async_computation | async-start | bytes 2105344 | tf_op jit(solution)/shard_map/all_gather | solution.py:35
  7.9 222.4 %all-gather.7.cloned.1.call-start = ((), (), s32[]{:S(2)}) async-start(), calls=%async_computation.1 | async-start | bytes 2105344 | tf_op jit(solution)/shard_map/all_gather | solution.py:35
  127.0 213.8 %all-gather.9.cloned.1.call-start = ((), (), s32[]{:S(2)}) async-start(), calls=%async_computation.2 | async-start | bytes 2105344 | tf_op jit(solution)/shard_map/all_gather | solution.py:35
  230.3 6.4 %copy-start = (f32[16,16,128]{2,1,0:T(8,128)S(1)}, f32[16,16,128]{2,1,0:T(8,128)}, u32[]{:S(2)}) copy-start(f32[16,16,128]{2,1,0:T(8,128)} %param.6) | copy-start | bytes 393220
  237.5 213.7 %all-gather.11.cloned.1.call-start = ((), (), s32[]{:S(2)}) async-start(), calls=%async_computation.3 | async-start | bytes 2105344 | tf_op jit(solution)/shard_map/all_gather | solution.py:35
  348.6 109.1 %copy-start.1 = (f32[16,128]{1,0:T(8,128)S(1)}, f32[16,128]{1,0:T(8,128)}, u32[]{:S(2)}) copy-start(f32[16,128]{1,0:T(8,128)} %fusion.8) | copy-start | bytes 24580
  348.6 109.1 %copy-start.2 = (f32[16,128]{1,0:T(8,128)S(1)}, f32[16,128]{1,0:T(8,128)}, u32[]{:S(2)}) copy-start(f32[16,128]{1,0:T(8,128)} %select_reduce_fusion.2) | copy-start | bytes 24580
  348.6 109.1 %copy-start.3 = (f32[16,128]{1,0:T(8,128)S(1)}, f32[16,128]{1,0:T(8,128)}, u32[]{:S(2)}) copy-start(f32[16,128]{1,0:T(8,128)} %select_reduce_fusion.1) | copy-start | bytes 24580
  348.6 109.1 %copy-start.4 = (f32[16,128]{1,0:T(8,128)S(1)}, f32[16,128]{1,0:T(8,128)}, u32[]{:S(2)}) copy-start(f32[16,128]{1,0:T(8,128)} %param.8) | copy-start | bytes 24580
Sparse Core Ops, SparseCore 0:
  11.7 108.2 all-gather.4
  127.1 103.1 all-gather.6
  237.6 103.1 all-gather.8
  348.0 103.1 all-gather.10
where the time goes:
time: 507 us; the launch traced here: 506 us
  waiting for transfers between devices  421 us (83%)
  blocking collectives  40.9 us (8%)
  matrix products  25.8 us (5%)
  between operations  14.6 us (3%)
    all_gather x4, waiting for transfers between devices, local(): field_all = lax.all_gather(unshifted, STATE, axis=0, tiled=True)  420 us
    pmax x4, blocking collectives, over_axes(): x = lax.pmax(x, axis)  40.9 us
    dot_general x4, matrix products, local(): jnp.dot(flat_rows, field_all, precision=lax.Precision.HIGHEST, preferred_...  25.8 us
  transfers between devices with their start and end apart: 4, of which 4 were waited for; matrix products, arithmetic and copies ran while one was open for 0% of the time, Pallas kernels for 0%

commit v1 on v0

v1 whole, which is shorter than its diff:
```python
import functools

import jax
import jax.numpy as jnp
from jax import lax
from jax.experimental import pallas as pl
from jax.experimental.pallas import tpu as pltpu
from jax.sharding import Mesh
from jax.sharding import PartitionSpec as P

ITERS = 4
YS, ZS, XS = 4, 8, 4
AXES = ("y", "z", "x", "c")
BIG = 1e30
MESH = pl.DeviceIdType.MESH


def ring(delta, size):
    return min(delta, size - delta)


PLANE = sorted(
    ((da, dz) for da in range(4) for dz in range(ZS) if da or dz),
    key=lambda d: (ring(d[0], 4) + ring(d[1], ZS), ring(d[1], ZS), d),
)
GROUPS = (0, 1, 3, 2)


def kernel(
    trans,
    costs,
    counts,
    start,
    ref_state,
    rel_out,
    low_out,
    up_out,
    values,
    raw,
    hi,
    lo,
    masked,
    cost2,
    right,
    total,
    swap,
    mine,
    plane_in,
    line_in,
    half_in,
    best_io,
    plane_recv,
    line_recv,
    plane_send,
    line_send,
    raw_sem,
    raw_send,
    raw_recv,
    pair_send,
    pair_recv,
):
    y, z, x, c = (lax.axis_index(a) for a in AXES)
    a = y + c * (x - y)
    b = x + c * (y - x)

    def wrap(i, size):
        return lax.rem(i + size, size)

    def place(a_, z_, b_):
        y_ = a_ + c * (b_ - a_)
        x_ = b_ + c * (a_ - b_)
        return y_, z_, x_

    partner = (y, z, x, 1 - c)

    quarter = 64
    loads = []
    for i in range(4):
        rows = pl.ds(i * quarter, quarter)
        copy = pltpu.make_async_copy(trans.at[rows], raw.at[0, rows], raw_sem.at[i])
        copy.start()
        loads.append(copy)

    barrier = pltpu.get_barrier_semaphore()
    for da, dz in PLANE:
        pl.semaphore_signal(
            barrier, inc=1, device_id=(*place(wrap(a + da, 4), wrap(z + dz, ZS), b), c), device_id_type=MESH
        )
    for db in (1, 3, 2):
        pl.semaphore_signal(
            barrier, inc=1, device_id=(*place(a, z, wrap(b + db, 4)), c), device_id_type=MESH
        )
    pl.semaphore_signal(barrier, inc=1, device_id=partner, device_id_type=MESH)

    lane = lax.broadcasted_iota(jnp.int32, (16, 128), 1)
    left = lane < 64
    action = lax.broadcasted_iota(jnp.int32, (16, 128), 0)
    for s in range(16):
        rows = pl.ds(s * 16, 16)
        masked[0, rows, :] = jnp.where(action < counts[s], costs[rows, :], jnp.float32(BIG))

    pl.semaphore_wait(barrier, len(PLANE) + 4)

    def to_partner(src, dst, k):
        copy = pltpu.make_async_remote_copy(
            src, dst, pair_send.at[k], pair_recv.at[k], device_id=partner, device_id_type=MESH
        )
        copy.start()
        return copy

    send_start = to_partner(start, swap.at[0], 0)
    send_cost = to_partner(masked.at[0], masked.at[1], 1)
    exchanges = []
    for i in range(4):
        rows = pl.ds(i * quarter, quarter)
        copy = pltpu.make_async_remote_copy(
            trans.at[rows],
            raw.at[1, rows],
            raw_send.at[i],
            raw_recv.at[i],
            device_id=partner,
            device_id_type=MESH,
        )
        copy.start()
        exchanges.append(copy)

    keep = jnp.logical_xor(left, c == 1)

    def both_halves(v):
        return jnp.where(keep[: v.shape[0]], v, pltpu.roll(v, 64, 1))

    send_start.wait_recv()
    own = both_halves(start[...])
    other = both_halves(swap[0])
    first = jnp.where(c == 0, own, other)
    second = jnp.where(c == 0, other, own)
    values[0, y, z, x] = jnp.where(left, first, second)

    def split_rows(which, base):
        def step(i, _):
            rows = pl.ds(pl.multiple_of(i * 16, 16), 16)
            out_rows = pl.ds(pl.multiple_of(base + i * 16, 16), 16)
            for g in range(4):
                v = raw[which, rows, g * 1024 : (g + 1) * 1024]
                h = v.astype(jnp.bfloat16)
                hi[g, out_rows, :] = h
                lo[g, out_rows, :] = (v - h.astype(jnp.float32)).astype(jnp.bfloat16)
            return 0

        lax.fori_loop(0, 16, step, 0)

    def scatter_plane(t):
        src = values.at[t, y, z, x]
        for da, dz in PLANE:
            pltpu.make_async_remote_copy(
                src,
                values.at[t, y, z, x],
                plane_send.at[t],
                plane_recv.at[t, da, dz],
                device_id=(*place(wrap(a + da, 4), wrap(z + dz, ZS), b), c),
                device_id_type=MESH,
            ).start()

    def forward(t, chunk, slab):
        for db in (2, 1, 3):
            pltpu.make_async_remote_copy(
                values.at[t, *chunk],
                values.at[t, *chunk],
                line_send.at[t],
                line_recv.at[t, db, slab],
                device_id=(*place(a, z, wrap(b + db, 4)), c),
                device_id_type=MESH,
            ).start()

    def relay(t):
        forward(t, (y, z, x), 0)
        for da, dz in PLANE:
            chunk = place(wrap(a - da, 4), wrap(z - dz, ZS), b)
            pltpu.make_async_remote_copy(
                values.at[t, *chunk],
                values.at[t, *chunk],
                plane_send.at[t],
                plane_recv.at[t, da, dz],
                device_id=partner,
                device_id_type=MESH,
            ).wait_recv()
            forward(t, chunk, (4 - da) % 4)

    def wait_slab(t, db, da):
        ref = values.at[t, 0, :, 0]
        pltpu.make_async_copy(ref, ref, line_recv.at[t, db, da]).wait()

    def multiply(t, g, base, first_group):
        y_ = wrap(y + g, 4)
        v = values[t, y_].reshape(32 * 16, 128) - base
        h = v.astype(jnp.bfloat16).astype(jnp.float32)
        r = v - h
        l_ = lax.broadcasted_iota(jnp.int32, v.shape, 1) < 64
        turned = pltpu.roll(jnp.where(l_, r, h), 64, 1)
        top = jnp.where(l_, h, turned).astype(jnp.bfloat16).reshape(32, 1, 16, 128)
        bottom = jnp.where(l_, turned, r).astype(jnp.bfloat16).reshape(32, 1, 16, 128)
        right[...] = jnp.concatenate([top, bottom], axis=1).reshape(1024, 128)
        w = right[...]
        part = jnp.dot(hi[y_], w, preferred_element_type=jnp.float32)
        part += jnp.dot(lo[y_], w, preferred_element_type=jnp.float32)
        if first_group:
            total[...] = part
        else:
            total[...] += part

    def finish_costs():
        send_cost.wait_recv()

        def step(i, _):
            for which in range(2):
                rows = pl.ds(pl.multiple_of(i * 16, 16), 16)
                base = (c if which == 0 else 1 - c) * 256
                cost2[pl.ds(pl.multiple_of(base + i * 16, 16), 16), :] = both_halves(masked[which, rows, :])
            return 0

        lax.fori_loop(0, 16, step, 0)

    mine[0] = jnp.full((8, 128), -BIG, jnp.float32)
    row8 = lax.broadcasted_iota(jnp.int32, (8, 128), 0)
    lane8 = lax.broadcasted_iota(jnp.int32, (8, 128), 1)

    def iteration(t, _):
        scatter_plane(t)

        @pl.when(t == 0)
        def _():
            for copy in loads:
                copy.wait()
            split_rows(0, c * 256)

        relay(t)

        @pl.when(t == 0)
        def _():
            finish_costs()
            for copy in exchanges:
                copy.wait_recv()
            split_rows(1, (1 - c) * 256)

        packed = values[t, y, z, x]
        base = packed[0:1, :]
        base = jnp.where(lax.broadcasted_iota(jnp.int32, (1, 128), 1) < 64, base, pltpu.roll(base, 64, 1))

        for k, g in enumerate(GROUPS):

            @pl.when(c == 0)
            def _():
                for db in (1, 3, 2):
                    wait_slab(t, db, g)

            if g:

                @pl.when(c == 1)
                def _():
                    for da in range(4):
                        wait_slab(t, 4 - g, da)

            multiply(t, g, base, k == 0)

        e = total[...]
        q = e + pltpu.roll(e, 64, 1) + cost2[...]
        best = jnp.min(q.reshape(32, 16, 128), axis=1) + base
        best_io[0] = best[:16]
        best_io[1] = best[16:]
        new = jnp.where(left, best[:16], best[16:])
        values[t + 1, y, z, x] = new
        inc = new - packed
        up = jnp.max(inc, axis=0, keepdims=True)
        down = jnp.max(-inc, axis=0, keepdims=True)
        up = jnp.maximum(up, pltpu.roll(up, 64, 1))
        down = jnp.maximum(down, pltpu.roll(down, 64, 1))
        mine[0] = jnp.where(row8 == t, jnp.where(lane8 < 64, up, down), mine[0])

        chunks = values.at[t, :, :, 0]
        pltpu.make_async_copy(chunks, chunks, line_send.at[t]).wait()
        pltpu.make_async_copy(chunks, chunks, line_send.at[t]).wait()
        pltpu.make_async_copy(chunks, chunks, line_send.at[t]).wait()
        for part in (values.at[t, 0:3, :, 0], values.at[t, 0, 0:7, 0]):
            pltpu.make_async_copy(part, part, plane_send.at[t]).wait()
        return 0

    lax.fori_loop(0, ITERS, iteration, 0)

    device = (y * ZS + z) * XS + x
    ids = device * 32 + lax.broadcasted_iota(jnp.int32, (16, 128), 0)
    picked = jnp.maximum(
        jnp.where(ids == ref_state[0], best_io[0], -BIG), jnp.where(ids + 16 == ref_state[0], best_io[1], -BIG)
    )
    ref_row = jnp.max(picked, axis=0, keepdims=True)
    mine[0] = jnp.where(row8 == 4, ref_row, mine[0])
    send_best = to_partner(best_io.at[1 - c], swap.at[1], 2)

    for da, dz in PLANE:
        pltpu.make_async_remote_copy(
            mine.at[0],
            plane_in.at[da, dz],
            plane_send.at[4],
            plane_recv.at[4, da, dz],
            device_id=(*place(wrap(a + da, 4), wrap(z + dz, ZS), b), c),
            device_id_type=MESH,
        ).start()
    top = mine[0]
    for da, dz in PLANE:
        pltpu.make_async_remote_copy(
            mine.at[0],
            plane_in.at[da, dz],
            plane_send.at[4],
            plane_recv.at[4, da, dz],
            device_id=partner,
            device_id_type=MESH,
        ).wait_recv()
        top = jnp.maximum(top, plane_in[da, dz])
    mine[1] = top
    lines = []
    for db in (2, 1, 3):
        copy = pltpu.make_async_remote_copy(
            mine.at[1],
            line_in.at[db],
            line_send.at[4],
            line_recv.at[4, db, 0],
            device_id=(*place(a, z, wrap(b + db, 4)), c),
            device_id_type=MESH,
        )
        copy.start()
        lines.append((copy, db))
    for copy, db in lines:
        copy.wait_recv()
        top = jnp.maximum(top, line_in[db])
    half_in[0] = top
    send_half = to_partner(half_in.at[0], half_in.at[1], 3)
    send_half.wait_recv()
    other = half_in[1]
    r0 = jnp.where(c == 0, top, other)
    r1 = jnp.where(c == 0, other, top)
    left8 = lane8 < 64
    upper = jnp.where(left8, r0, pltpu.roll(r1, 64, 1))
    lower = -jnp.where(left8, pltpu.roll(r0, 64, 1), r1)
    ref_full = jnp.where(left8, r0, r1)[4:5]
    up_out[...] = upper[0:4]
    low_out[...] = lower[0:4]
    send_best.wait_recv()
    rel_out[...] = jnp.where(keep, jnp.where(c == 0, best_io[0], best_io[1]), swap[1]) - ref_full

    part = plane_in.at[0:3]
    pltpu.make_async_copy(part, part, plane_send.at[4]).wait()
    part = plane_in.at[0, 0:7]
    pltpu.make_async_copy(part, part, plane_send.at[4]).wait()
    part = line_in.at[0:3]
    pltpu.make_async_copy(part, part, line_send.at[4]).wait()
    for copy in (send_start, send_cost, send_best, send_half, *exchanges):
        copy.wait_send()


def local(transitions, costs, valid_counts, start_values, ref_state):
    dma = pltpu.SemaphoreType.DMA
    f32, bf16 = jnp.float32, jnp.bfloat16
    vmem = pl.BlockSpec(memory_space=pltpu.VMEM)
    smem = pl.BlockSpec(memory_space=pltpu.SMEM)
    return pl.pallas_call(
        kernel,
        out_shape=(
            jax.ShapeDtypeStruct((16, 128), f32),
            jax.ShapeDtypeStruct((ITERS, 128), f32),
            jax.ShapeDtypeStruct((ITERS, 128), f32),
        ),
        in_specs=[pl.BlockSpec(memory_space=pl.ANY), vmem, smem, vmem, smem],
        out_specs=(vmem, vmem, vmem),
        scratch_shapes=[
            pltpu.VMEM((ITERS + 1, YS, ZS, XS, 16, 128), f32),
            pltpu.VMEM((2, 256, 4096), f32),
            pltpu.VMEM((4, 512, 1024), bf16),
            pltpu.VMEM((4, 512, 1024), bf16),
            pltpu.VMEM((2, 256, 128), f32),
            pltpu.VMEM((512, 128), f32),
            pltpu.VMEM((1024, 128), bf16),
            pltpu.VMEM((512, 128), f32),
            pltpu.VMEM((2, 16, 128), f32),
            pltpu.VMEM((2, 8, 128), f32),
            pltpu.VMEM((4, ZS, 8, 128), f32),
            pltpu.VMEM((4, 8, 128), f32),
            pltpu.VMEM((2, 8, 128), f32),
            pltpu.VMEM((2, 16, 128), f32),
            dma((ITERS + 1, 4, ZS)),
            dma((ITERS + 1, 4, 4)),
            dma((ITERS + 1,)),
            dma((ITERS + 1,)),
            dma((4,)),
            dma((4,)),
            dma((4,)),
            dma((4,)),
            dma((4,)),
        ],
        compiler_params=pltpu.CompilerParams(
            collective_id=0, has_side_effects=True, vmem_limit_bytes=60 * 1024 * 1024
        ),
        name="value_iteration",
    )(
        transitions.reshape(256, 4096),
        costs.reshape(256, 128),
        valid_counts,
        start_values,
        ref_state,
    )


def solution(mesh):
    split = Mesh(mesh.devices.reshape(YS, ZS, XS, 2), AXES)
    return jax.shard_map(
        local,
        mesh=split,
        in_specs=(P(AXES, None, None), P(AXES, None, None), P(AXES), P(AXES, None), P()),
        out_specs=(P(AXES, None), P(), P()),
        check_vma=False,
    )
```

time: 507 us -> 102 us (0.20)
  waiting for transfers between devices: 421 us -> 0 us
  Pallas kernels: 0 us -> 97.1 us
  blocking collectives: 40.9 us -> 0 us
  matrix products: 25.8 us -> 0 us
  between operations: 14.6 us -> 1.29 us
    all_gather x4 -> x0, waiting for transfers between devices: 420 us -> none  [local(): field_all = lax.all_gather(unshifted, STATE, axis=0, tiled=True)]
    pallas_call x0 -> x1, Pallas kernels: none -> 97.1 us  [local(): pl.pallas_call(kernel, out_shape=(jax.ShapeDtypeStruct((16, 128), f32), j...]
    pmax x4 -> x0, blocking collectives: 40.9 us -> none  [over_axes(): x = lax.pmax(x, axis)]
    dot_general x4 -> x0, matrix products: 25.8 us -> none  [local(): jnp.dot(flat_rows, field_all, precision=lax.Precision.HIGHEST, preferred_...]
  transfers between devices with their start and end apart: 4 -> 0, of which waited for: 4 -> 0; matrix products, arithmetic and copies ran while one was open for 0% -> 0% of each run, Pallas kernels for 0% -> 0%
where the time goes in v1:
time: 102 us
  Pallas kernels  97.1 us (95%)
  local copies, waits for them, and re-layouts  3.77 us (4%)
  between operations  1.29 us (1%)
    pallas_call x1, Pallas kernels, local(): pl.pallas_call(kernel, out_shape=(jax.ShapeDtypeStruct((16, 128), f32), j...  97.1 us
    unnamed x3, local copies, waits for them, and re-layouts  3.77 us

profile of v1, /device:TPU:1, one launch (start us, length us, event | category | flops | bytes accessed | tf_op | source)
XLA Modules:
  0.0 102.1 jit_solution(2305326436845548811)
XLA Ops:
  1.3 97.1 %value_iteration.1 = (f32[16,128]{1,0:T(8,128)}, f32[4,128]{1,0:T(4,128)}, f32[4,128]{1,0:T(4,128)}) custom-call(f32[256,4096]{1,0:T(8,128)} %bitcast.2, f32[256,128]{1,0:T(8,128)} %bitcast.3, s32[16]{0:T(128)} %counts.1, f32[16,128]{1,0:T(8,128)} %start.1, s32[1]{0:T(128)S(6)} %copy.11.ref_state), custom_call_target="tpu_custom_call" | custom-call | tf_op jit(solution)/shard_map/value_iteration/pallas_call | solution.py:364
  98.4 1.3 %copy.12 = f32[16,128]{1,0:T(8,128)} copy(f32[16,128]{1,0:T(8,128)} %get-tuple-element.6) | data formatting | bytes 16384
  99.7 1.2 %copy.13 = f32[4,128]{1,0:T(4,128)} copy(f32[4,128]{1,0:T(4,128)} %get-tuple-element.7) | data formatting | bytes 4096
  100.9 1.2 %copy.14 = f32[4,128]{1,0:T(4,128)} copy(f32[4,128]{1,0:T(4,128)} %get-tuple-element.8) | data formatting | bytes 4096

commit v2 on v1

v2 whole, which is shorter than its diff:
```python
import functools

import jax
import jax.numpy as jnp
from jax import lax
from jax.experimental import pallas as pl
from jax.experimental.pallas import tpu as pltpu
from jax.sharding import Mesh
from jax.sharding import PartitionSpec as P

ITERS = 4
YS, ZS, XS = 4, 8, 4
AXES = ("y", "z", "x", "c")
BIG = 1e30
MESH = pl.DeviceIdType.MESH


def ring(delta, size):
    return min(delta, size - delta)


PLANE = sorted(
    ((da, dz) for da in range(4) for dz in range(ZS) if da or dz),
    key=lambda d: (ring(d[0], 4) + ring(d[1], ZS), ring(d[1], ZS), d),
)

TREE = (
    (0, (31, 32, 12, 25, 21, 20, 7, 4, 19, 91, 99, 105, 89, 34, 58, 28, 35, 40, 1, 96, 72, 125, 92, 107, 42, 3, 70, 100, 98, 2, 127)),
    (32, (64, 67, 63, 37, 65)),
    (4, (9, 38, 36, 69, 5, 102)),
    (28, (29, 60, 124)),
    (96, (97,)),
    (31, (26, 27, 95, 126, 30)),
    (7, (71, 10, 39, 6, 103, 11)),
    (1, (33,)),
    (99, (111,)),
    (12, (14, 44, 8, 15, 108, 13)),
    (100, (68,)),
    (20, (120, 24, 23, 56, 119, 55, 116, 16, 52)),
    (40, (41, 43)),
    (92, (88, 84)),
    (105, (109, 73, 106, 101, 110, 104, 113, 74)),
    (34, (66, 62, 94)),
    (21, (22, 117, 53, 54, 17, 118)),
    (72, (75, 77, 76)),
    (91, (79, 90, 59, 87, 123, 86, 80)),
    (89, (93, 85, 122, 81, 121, 57)),
    (19, (18, 112, 115, 51, 82, 49, 114, 48, 83)),
    (42, (78, 50, 47, 46)),
    (60, (61,)),
    (44, (45,)),
)
GROUPS = (
    (
        ((0, 0), (0, 1), (1, 0), (0, 7), (3, 0), (1, 1), (0, 6), (3, 7)),
        ((0, 2), (2, 7), (0, 5), (3, 6), (2, 0), (1, 7), (0, 3), (1, 6)),
        ((2, 2), (2, 6), (3, 2), (3, 3), (1, 5), (1, 3), (0, 4), (2, 1)),
        ((2, 3), (3, 1), (1, 2), (1, 4)),
        ((2, 4), (3, 4), (2, 5), (3, 5)),
    ),
    (
        ((0, 0), (0, 1), (1, 0), (3, 0), (1, 1), (0, 7), (1, 7), (2, 7)),
        ((2, 0), (3, 7), (0, 6), (3, 6), (1, 6), (0, 2), (0, 3), (0, 5)),
        ((1, 2), (1, 3), (2, 6), (2, 1), (3, 3), (3, 2), (2, 3), (3, 1)),
        ((2, 2), (1, 4), (2, 4), (0, 4)),
        ((1, 5), (3, 4), (2, 5), (3, 5)),
    ),
)


def parts(d):
    return d // 32, d // 4 % ZS, d % 4


def step(d, p):
    return tuple((i - j) % n for i, j, n in zip(parts(d), parts(p), (4, ZS, 4)))


HOLDERS = {p: i for i, (p, _) in enumerate(TREE)}
LINE = ((0, 0, 2), (0, 0, 1), (0, 0, 3))
PARTNERS = sorted(
    {step(d, p) for p, receivers in TREE for d in receivers} | {(da, dz, 0) for da, dz in PLANE} | set(LINE)
)
PARTNERS = sorted(set(PARTNERS) | {tuple(-i % n for i, n in zip(e, (4, ZS, 4))) for e in PARTNERS})


def group_of(d, c):
    a, z, b = step(0, d)
    block = (a if c == 0 else b, z)
    return next(i for i, g in enumerate(GROUPS[c]) if block in g)


LEAVES = [d for d in range(1, 128) if d not in HOLDERS]


def kernel(
    trans,
    costs_in,
    counts_in,
    start_in,
    ref_in,
    out,
    values,
    costs,
    counts,
    start,
    ref_state,
    raw,
    hi,
    lo,
    masked,
    cost2,
    total,
    swap,
    mine,
    plane_in,
    line_in,
    half_in,
    best_io,
    hold_recv,
    leaf_recv,
    plane_recv,
    line_recv,
    send_sem,
    line_send,
    small_sem,
    raw_sem,
    raw_send,
    raw_recv,
    pair_send,
    pair_recv,
):
    y, z, x, c = (lax.axis_index(a) for a in AXES)
    a = y + c * (x - y)
    b = x + c * (y - x)

    def wrap(i, size):
        return lax.rem(i + size, size)

    def place(a_, z_, b_):
        y_ = a_ + c * (b_ - a_)
        x_ = b_ + c * (a_ - b_)
        return y_, z_, x_

    partner = (y, z, x, 1 - c)
    here = (y * ZS + z) * XS + x

    def member(da, dz, db):
        return (*place(wrap(a + da, 4), wrap(z + dz, ZS), wrap(b + db, 4)), c)

    def source(d):
        da, dz, db = parts(d)
        y_, z_, x_ = place(wrap(a - da, 4), wrap(z - dz, ZS), wrap(b - db, 4))
        return (y_ * ZS + z_) * XS + x_

    small = []
    for i, (src, dst) in enumerate(
        ((start_in, start), (costs_in, costs), (counts_in, counts), (ref_in, ref_state))
    ):
        copy = pltpu.make_async_copy(src, dst, small_sem.at[i])
        copy.start()
        small.append(copy)
    quarter = 64
    loads = []
    for i in range(4):
        rows = pl.ds(i * quarter, quarter)
        copy = pltpu.make_async_copy(trans.at[rows], raw.at[0, rows], raw_sem.at[i])
        copy.start()
        loads.append(copy)

    barrier = pltpu.get_barrier_semaphore()
    for e in PARTNERS:
        pl.semaphore_signal(barrier, inc=1, device_id=member(*e), device_id_type=MESH)
    pl.semaphore_signal(barrier, inc=1, device_id=partner, device_id_type=MESH)

    lane = lax.broadcasted_iota(jnp.int32, (16, 128), 1)
    left = lane < 64
    action = lax.broadcasted_iota(jnp.int32, (16, 128), 0)
    for copy in small:
        copy.wait()
    for s in range(16):
        rows = pl.ds(s * 16, 16)
        masked[0, rows, :] = jnp.where(action < counts[s], costs[rows, :], jnp.float32(BIG))

    pl.semaphore_wait(barrier, len(PARTNERS) + 1)

    def to_partner(src, dst, k):
        copy = pltpu.make_async_remote_copy(
            src, dst, pair_send.at[k], pair_recv.at[k], device_id=partner, device_id_type=MESH
        )
        copy.start()
        return copy

    send_start = to_partner(start, swap.at[0], 0)
    send_cost = to_partner(masked.at[0], masked.at[1], 1)
    exchanges = []
    for i in range(4):
        rows = pl.ds(i * quarter, quarter)
        copy = pltpu.make_async_remote_copy(
            trans.at[rows],
            raw.at[1, rows],
            raw_send.at[i],
            raw_recv.at[i],
            device_id=partner,
            device_id_type=MESH,
        )
        copy.start()
        exchanges.append(copy)

    keep = jnp.logical_xor(left, c == 1)

    def both_halves(v):
        return jnp.where(keep[: v.shape[0]], v, pltpu.roll(v, 64, 1))

    send_start.wait_recv()
    left8 = lax.broadcasted_iota(jnp.int32, (8, 128), 1) < 64
    own = both_halves(start[...])
    other = both_halves(swap[0])
    own = jnp.where(left8, own[:8], own[8:])
    other = jnp.where(left8, other[:8], other[8:])
    values[0, here, 0:8, :] = jnp.where(c == 0, own, other)
    values[0, here, 8:16, :] = jnp.where(c == 0, other, own)

    def split_rows(which, base):
        def step(i, _):
            rows = pl.ds(pl.multiple_of(i * 16, 16), 16)
            out_rows = pl.ds(pl.multiple_of(base + i * 16, 16), 16)
            for g in range(32):
                v = raw[which, rows, g * 128 : (g + 1) * 128]
                h = v.astype(jnp.bfloat16)
                hi[g // ZS, g % ZS, out_rows, :] = h
                lo[g // ZS, g % ZS, out_rows, :] = (v - h.astype(jnp.float32)).astype(jnp.bfloat16)
            return 0

        lax.fori_loop(0, 16, step, 0)

    def receive_sem(t, d):
        if d in HOLDERS:
            return hold_recv.at[t, HOLDERS[d]]
        g0, g1 = group_of(d, 0), group_of(d, 1)
        return leaf_recv.at[t, g0 + c * (g1 - g0)]

    def hand_on(t, p, receivers):
        chunk = source(p)
        if p:
            wait_bytes(values.at[t, chunk], hold_recv.at[t, HOLDERS[p]])
        for d in receivers:
            pltpu.make_async_remote_copy(
                values.at[t, chunk],
                values.at[t, chunk],
                send_sem.at[t],
                receive_sem(t, d),
                device_id=member(*step(d, p)),
                device_id_type=MESH,
            ).start()

    def wait_bytes(ref, sem):
        pltpu.make_async_copy(ref, ref, sem).wait()

    def wait_group(t, i):
        for core in range(2):
            n = sum(group_of(d, core) == i for d in LEAVES)

            @pl.when(c == core)
            def _():
                if n:
                    wait_bytes(values.at[t, 0:n], leaf_recv.at[t, i])

    def multiply(t, i, base):
        blocks = []
        for (y0, z0), (y1, z1) in zip(GROUPS[0][i], GROUPS[1][i]):
            blocks.append((wrap(y + y0 + c * (y1 - y0), 4), wrap(z + z0 + c * (z1 - z0), ZS)))
        n = len(blocks)
        v = jnp.concatenate([values[t, pl.ds((k[0] * ZS + k[1]) * XS, XS)].reshape(64, 128) for k in blocks], axis=0) - base
        h = v.astype(jnp.bfloat16).astype(jnp.float32)
        r = v - h
        l_ = lax.broadcasted_iota(jnp.int32, v.shape, 1) < 64
        turned = pltpu.roll(jnp.where(l_, r, h), 64, 1)
        top = jnp.where(l_, h, turned).reshape(n * 8, 1, 8, 128)
        bottom = jnp.where(l_, turned, r).reshape(n * 8, 1, 8, 128)
        w = jnp.concatenate([top, bottom], axis=1).reshape(n * 128, 128).astype(jnp.bfloat16)
        rows = [half[k[0], k[1]] for half in (hi, lo) for k in blocks]
        part = jnp.dot(
            jnp.concatenate(rows, axis=1), jnp.concatenate([w, w], axis=0), preferred_element_type=jnp.float32
        )
        if i == 0:
            total[...] = part
        else:
            total[...] += part

    def finish_costs():
        send_cost.wait_recv()

        def step(i, _):
            for which in range(2):
                rows = pl.ds(pl.multiple_of(i * 16, 16), 16)
                base = (c if which == 0 else 1 - c) * 256
                cost2[pl.ds(pl.multiple_of(base + i * 16, 16), 16), :] = both_halves(masked[which, rows, :])
            return 0

        lax.fori_loop(0, 16, step, 0)

    mine[0] = jnp.full((8, 128), -BIG, jnp.float32)
    row8 = lax.broadcasted_iota(jnp.int32, (8, 128), 0)
    lane8 = lax.broadcasted_iota(jnp.int32, (8, 128), 1)

    def iteration(t, _):
        hand_on(t, *TREE[0])

        @pl.when(t == 0)
        def _():
            for copy in loads:
                copy.wait()
            split_rows(0, c * 256)

        for p, receivers in TREE[1:]:
            hand_on(t, p, receivers)

        @pl.when(t == 0)
        def _():
            finish_costs()
            for copy in exchanges:
                copy.wait_recv()
            split_rows(1, (1 - c) * 256)

        packed = values[t, here]
        base = packed[0:1, :]
        base = jnp.where(lax.broadcasted_iota(jnp.int32, (1, 128), 1) < 64, base, pltpu.roll(base, 64, 1))

        for i in range(len(GROUPS[0])):
            wait_group(t, i)
            multiply(t, i, base)

        e = total[...]
        q = e + pltpu.roll(e, 64, 1) + cost2[...]
        best = jnp.min(q.reshape(32, 16, 128), axis=1) + base
        best_io[0] = best[:16]
        best_io[1] = best[16:]
        new = jnp.concatenate(
            [jnp.where(left8, best[0:8], best[8:16]), jnp.where(left8, best[16:24], best[24:32])], axis=0
        )
        values[t + 1, here] = new
        inc = new - packed
        up = jnp.max(inc, axis=0, keepdims=True)
        down = jnp.max(-inc, axis=0, keepdims=True)
        up = jnp.maximum(up, pltpu.roll(up, 64, 1))
        down = jnp.maximum(down, pltpu.roll(down, 64, 1))
        mine[0] = jnp.where(row8 == t, jnp.where(lane8 < 64, up, down), mine[0])

        return 0

    lax.fori_loop(0, ITERS, iteration, 0)

    device = (y * ZS + z) * XS + x
    ids = device * 32 + lax.broadcasted_iota(jnp.int32, (16, 128), 0)
    picked = jnp.maximum(
        jnp.where(ids == ref_state[0], best_io[0], -BIG), jnp.where(ids + 16 == ref_state[0], best_io[1], -BIG)
    )
    ref_row = jnp.max(picked, axis=0, keepdims=True)
    mine[0] = jnp.where(row8 == 4, ref_row, mine[0])
    send_best = to_partner(best_io.at[1 - c], swap.at[1], 2)

    for da, dz in PLANE:
        pltpu.make_async_remote_copy(
            mine.at[0],
            plane_in.at[da * ZS + dz - 1],
            send_sem.at[4],
            plane_recv.at[da * ZS + dz - 1],
            device_id=member(da, dz, 0),
            device_id_type=MESH,
        ).start()
    top = mine[0]
    for da, dz in PLANE:
        pltpu.make_async_remote_copy(
            mine.at[0],
            plane_in.at[da * ZS + dz - 1],
            send_sem.at[4],
            plane_recv.at[da * ZS + dz - 1],
            device_id=partner,
            device_id_type=MESH,
        ).wait_recv()
        top = jnp.maximum(top, plane_in[da * ZS + dz - 1])
    mine[1] = top
    lines = []
    for db in (2, 1, 3):
        copy = pltpu.make_async_remote_copy(
            mine.at[1],
            line_in.at[db],
            line_send.at[0],
            line_recv.at[db],
            device_id=member(0, 0, db),
            device_id_type=MESH,
        )
        copy.start()
        lines.append((copy, db))
    for copy, db in lines:
        copy.wait_recv()
        top = jnp.maximum(top, line_in[db])
    half_in[0] = top
    send_half = to_partner(half_in.at[0], half_in.at[1], 3)
    send_half.wait_recv()
    other = half_in[1]
    r0 = jnp.where(c == 0, top, other)
    r1 = jnp.where(c == 0, other, top)
    upper = jnp.where(left8, r0, pltpu.roll(r1, 64, 1))
    lower = -jnp.where(left8, pltpu.roll(r0, 64, 1), r1)
    ref_full = jnp.where(left8, r0, r1)[4:5]
    out[16:20, :] = upper[0:4]
    out[20:24, :] = lower[0:4]
    send_best.wait_recv()
    out[0:16, :] = jnp.where(keep, jnp.where(c == 0, best_io[0], best_io[1]), swap[1]) - ref_full

    def sent(t, _):
        wait_bytes(values.at[t, 0:127], send_sem.at[t])
        return 0

    lax.fori_loop(0, ITERS, sent, 0)
    wait_bytes(plane_in.at[0:31], send_sem.at[4])
    part = line_in.at[0:3]
    pltpu.make_async_copy(part, part, line_send.at[0]).wait()
    for copy in (send_start, send_cost, send_best, send_half, *exchanges):
        copy.wait_send()


def deal(out, relative, lower, upper):
    relative[...] = out[0:16, :]
    upper[...] = out[16:20, :]
    lower[...] = out[20:24, :]


def local(transitions, costs, valid_counts, start_values, ref_state):
    dma = pltpu.SemaphoreType.DMA
    f32, bf16 = jnp.float32, jnp.bfloat16
    vmem = pl.BlockSpec(memory_space=pltpu.VMEM)
    out = pl.pallas_call(
        kernel,
        out_shape=jax.ShapeDtypeStruct((24, 128), f32),
        in_specs=[pl.BlockSpec(memory_space=pl.ANY)] * 5,
        out_specs=vmem,
        scratch_shapes=[
            pltpu.VMEM((ITERS + 1, YS * ZS * XS, 16, 128), f32),
            pltpu.VMEM((256, 128), f32),
            pltpu.SMEM((16,), jnp.int32),
            pltpu.VMEM((16, 128), f32),
            pltpu.SMEM((1,), jnp.int32),
            pltpu.VMEM((2, 256, 4096), f32),
            pltpu.VMEM((YS, ZS, 512, 128), bf16),
            pltpu.VMEM((YS, ZS, 512, 128), bf16),
            pltpu.VMEM((2, 256, 128), f32),
            pltpu.VMEM((512, 128), f32),
            pltpu.VMEM((512, 128), f32),
            pltpu.VMEM((2, 16, 128), f32),
            pltpu.VMEM((2, 8, 128), f32),
            pltpu.VMEM((4 * ZS - 1, 8, 128), f32),
            pltpu.VMEM((4, 8, 128), f32),
            pltpu.VMEM((2, 8, 128), f32),
            pltpu.VMEM((2, 16, 128), f32),
            dma((ITERS, len(TREE))),
            dma((ITERS, len(GROUPS[0]))),
            dma((4 * ZS - 1,)),
            dma((4,)),
            dma((ITERS + 1,)),
            dma((1,)),
            dma((4,)),
            dma((4,)),
            dma((4,)),
            dma((4,)),
            dma((4,)),
            dma((4,)),
        ],
        compiler_params=pltpu.CompilerParams(
            collective_id=0, has_side_effects=True, vmem_limit_bytes=60 * 1024 * 1024
        ),
        name="value_iteration",
    )(
        transitions.reshape(256, 4096),
        costs.reshape(256, 128),
        valid_counts,
        start_values,
        ref_state,
    )
    return pl.pallas_call(
        deal,
        out_shape=(
            jax.ShapeDtypeStruct((16, 128), f32),
            jax.ShapeDtypeStruct((ITERS, 128), f32),
            jax.ShapeDtypeStruct((ITERS, 128), f32),
        ),
        in_specs=[vmem],
        out_specs=(vmem, vmem, vmem),
        name="deal",
    )(out)


def solution(mesh):
    split = Mesh(mesh.devices.reshape(YS, ZS, XS, 2), AXES)
    return jax.shard_map(
        local,
        mesh=split,
        in_specs=(P(AXES, None, None), P(AXES, None, None), P(AXES), P(AXES, None), P()),
        out_specs=(P(AXES, None), P(), P()),
        check_vma=False,
    )
```

time: 102 us -> 88.6 us (0.87)
  Pallas kernels: 97.1 us -> 87.1 us
  local copies, waits for them, and re-layouts: 3.77 us -> 0 us
    pallas_call x1 -> x2, Pallas kernels: 97.1 us -> 87.1 us  [the longest x1 85.8 us: local(): pl.pallas_call(kernel, out_shape=jax.ShapeDtypeStruct((24, 128), f32), in...]
    unnamed x3 -> x0, local copies, waits for them, and re-layouts: 3.77 us -> none
where the time goes in v2:
time: 88.6 us; the launch traced here: 88.4 us
  Pallas kernels  87.1 us (98%)
  between operations  1.29 us (1%)
    pallas_call x1, Pallas kernels, local(): pl.pallas_call(kernel, out_shape=jax.ShapeDtypeStruct((24, 128), f32), in...  85.8 us

profile of v2, /device:TPU:1, one launch (start us, length us, event | category | flops | bytes accessed | tf_op | source)
XLA Modules:
  0.0 88.4 jit_solution(10909793064612336307)
XLA Ops:
  1.3 85.8 %value_iteration.1.out = f32[24,128]{1,0:T(8,128)} custom-call(f32[256,4096]{1,0:T(8,128)} %bitcast.2, f32[256,128]{1,0:T(8,128)} %bitcast.3, s32[16]{0:T(128)} %counts_in.1, f32[16,128]{1,0:T(8,128)} %start_in.1, s32[1]{0:T(128)S(6)} %copy.8.ref_in), custom_call_target="tpu_custom_call" | custom-call | tf_op jit(solution)/shard_map/value_iteration/pallas_call | solution.py:435
  87.1 1.3 %deal.1 = (f32[16,128]{1,0:T(8,128)}, f32[4,128]{1,0:T(4,128)}, f32[4,128]{1,0:T(4,128)}) custom-call(f32[24,128]{1,0:T(8,128)} %value_iteration.1.out), custom_call_target="tpu_custom_call" | custom-call | tf_op jit(solution)/shard_map/deal/pallas_call | solution.py:482

commit v3 on v2

--- a/solution.py
+++ b/solution.py
@@ -52,16 +52,14 @@
 )
 GROUPS = (
     (
-        ((0, 0), (0, 1), (1, 0), (0, 7), (3, 0), (1, 1), (0, 6), (3, 7)),
-        ((0, 2), (2, 7), (0, 5), (3, 6), (2, 0), (1, 7), (0, 3), (1, 6)),
-        ((2, 2), (2, 6), (3, 2), (3, 3), (1, 5), (1, 3), (0, 4), (2, 1)),
+        ((0, 0), (0, 1), (1, 0), (0, 7), (3, 0), (1, 1), (0, 6), (3, 7), (0, 2), (2, 7), (0, 5), (3, 6)),
+        ((2, 0), (1, 7), (0, 3), (1, 6), (2, 2), (2, 6), (3, 2), (3, 3), (1, 5), (1, 3), (0, 4), (2, 1)),
         ((2, 3), (3, 1), (1, 2), (1, 4)),
         ((2, 4), (3, 4), (2, 5), (3, 5)),
     ),
     (
-        ((0, 0), (0, 1), (1, 0), (3, 0), (1, 1), (0, 7), (1, 7), (2, 7)),
-        ((2, 0), (3, 7), (0, 6), (3, 6), (1, 6), (0, 2), (0, 3), (0, 5)),
-        ((1, 2), (1, 3), (2, 6), (2, 1), (3, 3), (3, 2), (2, 3), (3, 1)),
+        ((0, 0), (0, 1), (1, 0), (3, 0), (1, 1), (0, 7), (1, 7), (2, 7), (2, 0), (3, 7), (0, 6), (3, 6)),
+        ((1, 6), (0, 2), (0, 3), (0, 5), (1, 2), (1, 3), (2, 6), (2, 1), (3, 3), (3, 2), (2, 3), (3, 1)),
         ((2, 2), (1, 4), (2, 4), (0, 4)),
         ((1, 5), (3, 4), (2, 5), (3, 5)),
     ),
@@ -115,7 +113,7 @@
     mine,
     plane_in,
     line_in,
-    half_in,
+    bounds,
     best_io,
     hold_recv,
     leaf_recv,
@@ -148,6 +146,9 @@
     def member(da, dz, db):
         return (*place(wrap(a + da, 4), wrap(z + dz, ZS), wrap(b + db, 4)), c)
 
+    def other_core(da, dz, db):
+        return (*place(wrap(a + da, 4), wrap(z + dz, ZS), wrap(b + db, 4)), 1 - c)
+
     def source(d):
         da, dz, db = parts(d)
         y_, z_, x_ = place(wrap(a - da, 4), wrap(z - dz, ZS), wrap(b - db, 4))
@@ -172,6 +173,9 @@
     for e in PARTNERS:
         pl.semaphore_signal(barrier, inc=1, device_id=member(*e), device_id_type=MESH)
     pl.semaphore_signal(barrier, inc=1, device_id=partner, device_id_type=MESH)
+    for e in LINE:
+        pl.semaphore_signal(barrier, inc=1, device_id=other_core(*e), device_id_type=MESH)
+        pl.semaphore_signal(barrier, inc=1, device_id=other_core(*e[::-1]), device_id_type=MESH)
 
     lane = lax.broadcasted_iota(jnp.int32, (16, 128), 1)
     left = lane < 64
@@ -182,7 +186,7 @@
         rows = pl.ds(s * 16, 16)
         masked[0, rows, :] = jnp.where(action < counts[s], costs[rows, :], jnp.float32(BIG))
 
-    pl.semaphore_wait(barrier, len(PARTNERS) + 1)
+    pl.semaphore_wait(barrier, len(PARTNERS) + 1 + 2 * len(LINE))
 
     def to_partner(src, dst, k):
         copy = pltpu.make_async_remote_copy(
@@ -300,7 +304,6 @@
 
         lax.fori_loop(0, 16, step, 0)
 
-    mine[0] = jnp.full((8, 128), -BIG, jnp.float32)
     row8 = lax.broadcasted_iota(jnp.int32, (8, 128), 0)
     lane8 = lax.broadcasted_iota(jnp.int32, (8, 128), 1)
 
@@ -340,13 +343,6 @@
             [jnp.where(left8, best[0:8], best[8:16]), jnp.where(left8, best[16:24], best[24:32])], axis=0
         )
         values[t + 1, here] = new
-        inc = new - packed
-        up = jnp.max(inc, axis=0, keepdims=True)
-        down = jnp.max(-inc, axis=0, keepdims=True)
-        up = jnp.maximum(up, pltpu.roll(up, 64, 1))
-        down = jnp.maximum(down, pltpu.roll(down, 64, 1))
-        mine[0] = jnp.where(row8 == t, jnp.where(lane8 < 64, up, down), mine[0])
-
         return 0
 
     lax.fori_loop(0, ITERS, iteration, 0)
@@ -357,7 +353,15 @@
         jnp.where(ids == ref_state[0], best_io[0], -BIG), jnp.where(ids + 16 == ref_state[0], best_io[1], -BIG)
     )
     ref_row = jnp.max(picked, axis=0, keepdims=True)
-    mine[0] = jnp.where(row8 == 4, ref_row, mine[0])
+
+    def bounds_of(inc):
+        up = jnp.max(inc, axis=0, keepdims=True)
+        down = jnp.max(-inc, axis=0, keepdims=True)
+        up = jnp.maximum(up, pltpu.roll(up, 64, 1))
+        down = jnp.maximum(down, pltpu.roll(down, 64, 1))
+        return jnp.where(lane8[:1] < 64, up, down)
+
+    mine[0] = jnp.concatenate([bounds_of(values[ITERS, here] - values[ITERS - 1, here]), ref_row], axis=0)
     send_best = to_partner(best_io.at[1 - c], swap.at[1], 2)
 
     for da, dz in PLANE:
@@ -369,6 +373,27 @@
             device_id=member(da, dz, 0),
             device_id_type=MESH,
         ).start()
+
+    def increases(t, _):
+        def block(i, carry):
+            up, down = carry
+            chunks = pl.ds(pl.multiple_of(i * 8, 8), 8)
+            inc = values[t + 1, chunks] - values[t, chunks]
+            inc = inc.reshape(16, 8, 128)
+            return jnp.maximum(up, jnp.max(inc, axis=0)), jnp.maximum(down, jnp.max(-inc, axis=0))
+
+        low = jnp.full((8, 128), -BIG, jnp.float32)
+        up, down = lax.fori_loop(0, YS * ZS * XS // 8, block, (low, low))
+        up = jnp.max(up, axis=0, keepdims=True)
+        down = jnp.max(down, axis=0, keepdims=True)
+        up = jnp.maximum(up, pltpu.roll(up, 64, 1))
+        down = jnp.maximum(down, pltpu.roll(down, 64, 1))
+        bounds[0] = jnp.where(row8 == t, jnp.where(lane8 < 64, up, down), bounds[0])
+        return 0
+
+    bounds[0] = jnp.full((8, 128), -BIG, jnp.float32)
+    lax.fori_loop(0, ITERS - 1, increases, 0)
+    send_bounds = to_partner(bounds.at[0], bounds.at[1], 3)
     top = mine[0]
     for da, dz in PLANE:
         pltpu.make_async_remote_copy(
@@ -383,28 +408,34 @@
     mine[1] = top
     lines = []
     for db in (2, 1, 3):
-        copy = pltpu.make_async_remote_copy(
-            mine.at[1],
-            line_in.at[db],
-            line_send.at[0],
-            line_recv.at[db],
-            device_id=member(0, 0, db),
-            device_id_type=MESH,
-        )
-        copy.start()
-        lines.append((copy, db))
-    for copy, db in lines:
+        for k, device in enumerate((other_core(0, 0, db), member(0, 0, db))):
+            copy = pltpu.make_async_remote_copy(
+                mine.at[1],
+                line_in.at[4 * k + db],
+                line_send.at[4 * k + db],
+                line_recv.at[4 * k + db],
+                device_id=device,
+                device_id_type=MESH,
+            )
+            copy.start()
+            lines.append(copy)
+    copy = pltpu.make_async_remote_copy(
+        mine.at[1], line_in.at[0], line_send.at[0], line_recv.at[0], device_id=partner, device_id_type=MESH
+    )
+    copy.start()
+    lines.append(copy)
+    for copy in lines:
         copy.wait_recv()
-        top = jnp.maximum(top, line_in[db])
-    half_in[0] = top
-    send_half = to_partner(half_in.at[0], half_in.at[1], 3)
-    send_half.wait_recv()
-    other = half_in[1]
-    r0 = jnp.where(c == 0, top, other)
-    r1 = jnp.where(c == 0, other, top)
+    other = jnp.maximum(jnp.maximum(line_in[0], line_in[1]), jnp.maximum(line_in[2], line_in[3]))
+    top = jnp.maximum(jnp.maximum(top, line_in[5]), jnp.maximum(line_in[6], line_in[7]))
+    send_bounds.wait_recv()
+    own_bounds = jnp.where(row8 == ITERS - 1, top[0:1], bounds[0])
+    other_bounds = jnp.where(row8 == ITERS - 1, other[0:1], bounds[1])
+    r0 = jnp.where(c == 0, own_bounds, other_bounds)
+    r1 = jnp.where(c == 0, other_bounds, own_bounds)
     upper = jnp.where(left8, r0, pltpu.roll(r1, 64, 1))
     lower = -jnp.where(left8, pltpu.roll(r0, 64, 1), r1)
-    ref_full = jnp.where(left8, r0, r1)[4:5]
+    ref_full = jnp.where(jnp.logical_xor(left8[:1], c == 1), top[1:2], other[1:2])
     out[16:20, :] = upper[0:4]
     out[20:24, :] = lower[0:4]
     send_best.wait_recv()
@@ -416,9 +447,7 @@
 
     lax.fori_loop(0, ITERS, sent, 0)
     wait_bytes(plane_in.at[0:31], send_sem.at[4])
-    part = line_in.at[0:3]
-    pltpu.make_async_copy(part, part, line_send.at[0]).wait()
-    for copy in (send_start, send_cost, send_best, send_half, *exchanges):
+    for copy in (send_start, send_cost, send_best, send_bounds, *lines, *exchanges):
         copy.wait_send()
 
 
@@ -450,17 +479,17 @@
             pltpu.VMEM((512, 128), f32),
             pltpu.VMEM((512, 128), f32),
             pltpu.VMEM((2, 16, 128), f32),
-            pltpu.VMEM((2, 8, 128), f32),
-            pltpu.VMEM((4 * ZS - 1, 8, 128), f32),
-            pltpu.VMEM((4, 8, 128), f32),
+            pltpu.VMEM((2, 2, 128), f32),
+            pltpu.VMEM((4 * ZS - 1, 2, 128), f32),
+            pltpu.VMEM((8, 2, 128), f32),
             pltpu.VMEM((2, 8, 128), f32),
             pltpu.VMEM((2, 16, 128), f32),
             dma((ITERS, len(TREE))),
             dma((ITERS, len(GROUPS[0]))),
             dma((4 * ZS - 1,)),
-            dma((4,)),
+            dma((8,)),
             dma((ITERS + 1,)),
-            dma((1,)),
+            dma((8,)),
             dma((4,)),
             dma((4,)),
             dma((4,)),

time: 88.6 us -> 85.6 us (0.966)
  Pallas kernels: 87.1 us -> 84.1 us
    pallas_call x1, Pallas kernels: 85.8 us -> 82.8 us  [local(): pl.pallas_call(kernel, out_shape=jax.ShapeDtypeStruct((24, 128), f32), in...]
where the time goes in v3:
time: 85.6 us; the launch traced here: 85.4 us
  Pallas kernels  84.1 us (98%)
  between operations  1.29 us (2%)
    pallas_call x1, Pallas kernels, local(): pl.pallas_call(kernel, out_shape=jax.ShapeDtypeStruct((24, 128), f32), in...  82.8 us

profile of v3, /device:TPU:1, one launch (start us, length us, event | category | flops | bytes accessed | tf_op | source)
XLA Modules:
  0.0 85.4 jit_solution(8676811516352789862)
XLA Ops:
  1.3 82.8 %value_iteration.1.out = f32[24,128]{1,0:T(8,128)} custom-call(f32[256,4096]{1,0:T(8,128)} %bitcast.2, f32[256,128]{1,0:T(8,128)} %bitcast.3, s32[16]{0:T(128)} %counts_in.1, f32[16,128]{1,0:T(8,128)} %start_in.1, s32[1]{0:T(128)S(6)} %copy.8.ref_in), custom_call_target="tpu_custom_call" | custom-call | tf_op jit(solution)/shard_map/value_iteration/pallas_call | solution.py:464
  84.1 1.3 %deal.1 = (f32[16,128]{1,0:T(8,128)}, f32[4,128]{1,0:T(4,128)}, f32[4,128]{1,0:T(4,128)}) custom-call(f32[24,128]{1,0:T(8,128)} %value_iteration.1.out), custom_call_target="tpu_custom_call" | custom-call | tf_op jit(solution)/shard_map/deal/pallas_call | solution.py:511

commit v4 on v3

--- a/solution.py
+++ b/solution.py
@@ -25,43 +25,37 @@
 )
 
 TREE = (
-    (0, (31, 32, 12, 25, 21, 20, 7, 4, 19, 91, 99, 105, 89, 34, 58, 28, 35, 40, 1, 96, 72, 125, 92, 107, 42, 3, 70, 100, 98, 2, 127)),
-    (32, (64, 67, 63, 37, 65)),
-    (4, (9, 38, 36, 69, 5, 102)),
-    (28, (29, 60, 124)),
-    (96, (97,)),
-    (31, (26, 27, 95, 126, 30)),
-    (7, (71, 10, 39, 6, 103, 11)),
-    (1, (33,)),
-    (99, (111,)),
-    (12, (14, 44, 8, 15, 108, 13)),
-    (100, (68,)),
-    (20, (120, 24, 23, 56, 119, 55, 116, 16, 52)),
-    (40, (41, 43)),
-    (92, (88, 84)),
-    (105, (109, 73, 106, 101, 110, 104, 113, 74)),
-    (34, (66, 62, 94)),
-    (21, (22, 117, 53, 54, 17, 118)),
-    (72, (75, 77, 76)),
-    (91, (79, 90, 59, 87, 123, 86, 80)),
-    (89, (93, 85, 122, 81, 121, 57)),
-    (19, (18, 112, 115, 51, 82, 49, 114, 48, 83)),
-    (42, (78, 50, 47, 46)),
-    (60, (61,)),
-    (44, (45,)),
+    (0, (7, 20, 89, 4, 12, 31, 55, 70, 36, 8, 32, 27, 28, 64, 2, 91, 41, 117, 68, 88, 99, 97, 105, 35, 1, 98, 125, 38, 96, 44, 66, 127, 3, 112, 34, 33)),
+    (4, (10, 37, 15, 100, 103, 5)),
+    (32, (65, 60, 92, 67, 61)),
+    (28, (120, 124, 29)),
+    (7, (14, 39, 6, 11, 107)),
+    (31, (62, 30, 63)),
+    (20, (21, 25, 53, 118, 52, 24, 116, 23)),
+    (8, (9,)),
+    (12, (13,)),
+    (27, (22, 122, 59, 56, 26, 58, 18, 123, 119)),
+    (99, (95, 102)),
+    (68, (71, 72, 69, 104, 75)),
+    (89, (90, 85, 84, 94, 57)),
+    (41, (46, 73, 74, 40, 42, 49)),
+    (44, (43, 76, 47, 45, 79)),
+    (125, (121, 93, 126)),
+    (55, (82, 50, 54, 19, 51, 86, 87)),
+    (105, (101, 110, 109, 106, 77)),
+    (112, (16, 111, 81, 48, 80, 17, 114, 83, 108, 115, 113)),
+    (70, (78,)),
 )
 GROUPS = (
     (
-        ((0, 0), (0, 1), (1, 0), (0, 7), (3, 0), (1, 1), (0, 6), (3, 7), (0, 2), (2, 7), (0, 5), (3, 6)),
-        ((2, 0), (1, 7), (0, 3), (1, 6), (2, 2), (2, 6), (3, 2), (3, 3), (1, 5), (1, 3), (0, 4), (2, 1)),
-        ((2, 3), (3, 1), (1, 2), (1, 4)),
-        ((2, 4), (3, 4), (2, 5), (3, 5)),
+        ((0, 0), (1, 0), (3, 0), (0, 7), (3, 7), (0, 1), (2, 0), (0, 6), (0, 2), (2, 2), (3, 1), (0, 5)),
+        ((2, 7), (0, 3), (1, 2), (1, 1), (3, 5), (1, 6), (3, 2), (1, 7), (3, 3), (2, 1), (1, 3), (2, 6)),
+        ((3, 6), (1, 4), (2, 3), (0, 4), (3, 4), (1, 5), (2, 5), (2, 4)),
     ),
     (
-        ((0, 0), (0, 1), (1, 0), (3, 0), (1, 1), (0, 7), (1, 7), (2, 7), (2, 0), (3, 7), (0, 6), (3, 6)),
-        ((1, 6), (0, 2), (0, 3), (0, 5), (1, 2), (1, 3), (2, 6), (2, 1), (3, 3), (3, 2), (2, 3), (3, 1)),
-        ((2, 2), (1, 4), (2, 4), (0, 4)),
-        ((1, 5), (3, 4), (2, 5), (3, 5)),
+        ((0, 0), (0, 7), (3, 0), (0, 1), (1, 0), (2, 0), (1, 2), (1, 7), (3, 3), (0, 2), (3, 6), (2, 7)),
+        ((3, 2), (2, 1), (0, 6), (2, 2), (3, 1), (3, 7), (1, 3), (1, 1), (2, 6), (0, 3), (0, 5), (1, 6)),
+        ((3, 5), (3, 4), (2, 3), (1, 4), (0, 4), (1, 5), (2, 5), (2, 4)),
     ),
 )
 
@@ -79,7 +73,10 @@
 PARTNERS = sorted(
     {step(d, p) for p, receivers in TREE for d in receivers} | {(da, dz, 0) for da, dz in PLANE} | set(LINE)
 )
-PARTNERS = sorted(set(PARTNERS) | {tuple(-i % n for i, n in zip(e, (4, ZS, 4))) for e in PARTNERS})
+PARTNERS = sorted(
+    set(PARTNERS) | {tuple(-i % n for i, n in zip(e, (4, ZS, 4))) for e in PARTNERS},
+    key=lambda e: (-sum(ring(i, n) for i, n in zip(e, (4, ZS, 4))), e),
+)
 
 
 def group_of(d, c):
@@ -364,7 +361,7 @@
     mine[0] = jnp.concatenate([bounds_of(values[ITERS, here] - values[ITERS - 1, here]), ref_row], axis=0)
     send_best = to_partner(best_io.at[1 - c], swap.at[1], 2)
 
-    for da, dz in PLANE:
+    for da, dz in PLANE[::-1]:
         pltpu.make_async_remote_copy(
             mine.at[0],
             plane_in.at[da * ZS + dz - 1],

time: 85.6 us -> 84.2 us (0.984)
  Pallas kernels: 84.1 us -> 82.7 us
    pallas_call x1, Pallas kernels: 82.8 us -> 81.4 us  [local(): pl.pallas_call(kernel, out_shape=jax.ShapeDtypeStruct((24, 128), f32), in...]
where the time goes in v4:
time: 84.2 us; the launch traced here: 84 us
  Pallas kernels  82.7 us (98%)
  between operations  1.29 us (2%)
    pallas_call x1, Pallas kernels, local(): pl.pallas_call(kernel, out_shape=jax.ShapeDtypeStruct((24, 128), f32), in...  81.4 us

profile of v4, /device:TPU:1, one launch (start us, length us, event | category | flops | bytes accessed | tf_op | source)
XLA Modules:
  0.0 84.0 jit_solution(14198253097187848713)
XLA Ops:
  1.3 81.4 %value_iteration.1.out = f32[24,128]{1,0:T(8,128)} custom-call(f32[256,4096]{1,0:T(8,128)} %bitcast.2, f32[256,128]{1,0:T(8,128)} %bitcast.3, s32[16]{0:T(128)} %counts_in.1, f32[16,128]{1,0:T(8,128)} %start_in.1, s32[1]{0:T(128)S(6)} %copy.8.ref_in), custom_call_target="tpu_custom_call" | custom-call | tf_op jit(solution)/shard_map/value_iteration/pallas_call | solution.py:461
  82.7 1.3 %deal.1 = (f32[16,128]{1,0:T(8,128)}, f32[4,128]{1,0:T(4,128)}, f32[4,128]{1,0:T(4,128)}) custom-call(f32[24,128]{1,0:T(8,128)} %value_iteration.1.out), custom_call_target="tpu_custom_call" | custom-call | tf_op jit(solution)/shard_map/deal/pallas_call | solution.py:508

commit v5 on v4

--- a/solution.py
+++ b/solution.py
@@ -25,37 +25,41 @@
 )
 
 TREE = (
-    (0, (7, 20, 89, 4, 12, 31, 55, 70, 36, 8, 32, 27, 28, 64, 2, 91, 41, 117, 68, 88, 99, 97, 105, 35, 1, 98, 125, 38, 96, 44, 66, 127, 3, 112, 34, 33)),
-    (4, (10, 37, 15, 100, 103, 5)),
-    (32, (65, 60, 92, 67, 61)),
-    (28, (120, 124, 29)),
-    (7, (14, 39, 6, 11, 107)),
-    (31, (62, 30, 63)),
-    (20, (21, 25, 53, 118, 52, 24, 116, 23)),
-    (8, (9,)),
-    (12, (13,)),
-    (27, (22, 122, 59, 56, 26, 58, 18, 123, 119)),
-    (99, (95, 102)),
-    (68, (71, 72, 69, 104, 75)),
-    (89, (90, 85, 84, 94, 57)),
-    (41, (46, 73, 74, 40, 42, 49)),
-    (44, (43, 76, 47, 45, 79)),
-    (125, (121, 93, 126)),
-    (55, (82, 50, 54, 19, 51, 86, 87)),
-    (105, (101, 110, 109, 106, 77)),
-    (112, (16, 111, 81, 48, 80, 17, 114, 83, 108, 115, 113)),
-    (70, (78,)),
+    (0, (11, 1, 28, 92, 4, 13, 94, 36, 20, 75, 25, 32, 33, 101, 79, 123, 16, 35, 10, 66, 99, 70, 116, 2, 96, 3, 22, 64, 125, 97, 37, 103, 68, 31)),
+    (1, (34, 98, 30, 85, 65, 5)),
+    (28, (127, 124, 29, 60, 61, 95, 56)),
+    (4, (105, 69, 6, 100, 7, 102)),
+    (32, (62,)),
+    (96, (104, 67)),
+    (36, (71, 40, 38)),
+    (11, (106, 8, 111, 47, 15)),
+    (33, (93,)),
+    (20, (23, 24, 21)),
+    (35, (63, 59, 39)),
+    (25, (121, 26, 57, 58)),
+    (13, (73, 81, 45, 110, 12, 49, 14, 113, 9, 44, 17, 46, 77, 109)),
+    (116, (114, 118, 112, 120, 84, 115, 108, 117, 52)),
+    (123, (90, 88, 119, 122, 27, 87, 91)),
+    (75, (74, 43, 107, 72)),
+    (125, (126, 89)),
+    (37, (41,)),
+    (10, (42,)),
+    (79, (76, 83, 78, 80, 51, 82)),
+    (22, (50, 86, 18, 54)),
+    (56, (48, 55)),
+    (15, (19,)),
+    (21, (53,)),
 )
 GROUPS = (
     (
-        ((0, 0), (1, 0), (3, 0), (0, 7), (3, 7), (0, 1), (2, 0), (0, 6), (0, 2), (2, 2), (3, 1), (0, 5)),
-        ((2, 7), (0, 3), (1, 2), (1, 1), (3, 5), (1, 6), (3, 2), (1, 7), (3, 3), (2, 1), (1, 3), (2, 6)),
-        ((3, 6), (1, 4), (2, 3), (0, 4), (3, 4), (1, 5), (2, 5), (2, 4)),
+        ((0, 0), (3, 0), (0, 1), (1, 0), (0, 7), (2, 0), (0, 3), (2, 1), (3, 7), (0, 6)),
+        ((2, 7), (3, 1), (1, 7), (3, 2), (0, 5), (0, 2), (1, 2), (1, 6), (1, 1), (1, 5), (3, 5), (2, 6), (1, 3), (3, 6)),
+        ((2, 5), (1, 4), (2, 2), (2, 4), (2, 3), (0, 4), (3, 3), (3, 4)),
     ),
     (
-        ((0, 0), (0, 7), (3, 0), (0, 1), (1, 0), (2, 0), (1, 2), (1, 7), (3, 3), (0, 2), (3, 6), (2, 7)),
-        ((3, 2), (2, 1), (0, 6), (2, 2), (3, 1), (3, 7), (1, 3), (1, 1), (2, 6), (0, 3), (0, 5), (1, 6)),
-        ((3, 5), (3, 4), (2, 3), (1, 4), (0, 4), (1, 5), (2, 5), (2, 4)),
+        ((0, 0), (0, 1), (0, 7), (2, 0), (3, 0), (1, 0), (1, 1), (3, 1), (1, 7), (3, 7)),
+        ((2, 7), (1, 5), (0, 6), (2, 1), (1, 2), (3, 5), (3, 4), (1, 6), (3, 6), (2, 6), (0, 5), (2, 5), (0, 2), (0, 3)),
+        ((2, 2), (3, 2), (2, 3), (2, 4), (1, 3), (3, 3), (0, 4), (1, 4)),
     ),
 )
 

time: 84.2 us -> 82.7 us (0.982)
  Pallas kernels: 82.7 us -> 81.3 us
    pallas_call x1, Pallas kernels: 81.4 us -> 80 us  [local(): pl.pallas_call(kernel, out_shape=jax.ShapeDtypeStruct((24, 128), f32), in...]
where the time goes in v5:
time: 82.7 us; the launch traced here: 82.6 us
  Pallas kernels  81.3 us (98%)
  between operations  1.29 us (2%)
    pallas_call x1, Pallas kernels, local(): pl.pallas_call(kernel, out_shape=jax.ShapeDtypeStruct((24, 128), f32), in...  80 us

profile of v5, /device:TPU:1, one launch (start us, length us, event | category | flops | bytes accessed | tf_op | source)
XLA Modules:
  0.0 82.6 jit_solution(100314275593824598)
XLA Ops:
  1.3 80.0 %value_iteration.1.out = f32[24,128]{1,0:T(8,128)} custom-call(f32[256,4096]{1,0:T(8,128)} %bitcast.2, f32[256,128]{1,0:T(8,128)} %bitcast.3, s32[16]{0:T(128)} %counts_in.1, f32[16,128]{1,0:T(8,128)} %start_in.1, s32[1]{0:T(128)S(6)} %copy.8.ref_in), custom_call_target="tpu_custom_call" | custom-call | tf_op jit(solution)/shard_map/value_iteration/pallas_call | solution.py:465
  81.2 1.3 %deal.1 = (f32[16,128]{1,0:T(8,128)}, f32[4,128]{1,0:T(4,128)}, f32[4,128]{1,0:T(4,128)}) custom-call(f32[24,128]{1,0:T(8,128)} %value_iteration.1.out), custom_call_target="tpu_custom_call" | custom-call | tf_op jit(solution)/shard_map/deal/pallas_call | solution.py:512

commit v6 on v5

--- a/solution.py
+++ b/solution.py
@@ -52,13 +52,13 @@
 )
 GROUPS = (
     (
-        ((0, 0), (3, 0), (0, 1), (1, 0), (0, 7), (2, 0), (0, 3), (2, 1), (3, 7), (0, 6)),
-        ((2, 7), (3, 1), (1, 7), (3, 2), (0, 5), (0, 2), (1, 2), (1, 6), (1, 1), (1, 5), (3, 5), (2, 6), (1, 3), (3, 6)),
+        ((0, 0), (3, 0), (0, 1), (1, 0), (0, 7), (2, 0), (0, 3), (2, 1)),
+        ((3, 7), (0, 6), (2, 7), (3, 1), (1, 7), (3, 2), (0, 5), (0, 2), (1, 2), (1, 6), (1, 1), (1, 5), (3, 5), (2, 6), (1, 3), (3, 6)),
         ((2, 5), (1, 4), (2, 2), (2, 4), (2, 3), (0, 4), (3, 3), (3, 4)),
     ),
     (
-        ((0, 0), (0, 1), (0, 7), (2, 0), (3, 0), (1, 0), (1, 1), (3, 1), (1, 7), (3, 7)),
-        ((2, 7), (1, 5), (0, 6), (2, 1), (1, 2), (3, 5), (3, 4), (1, 6), (3, 6), (2, 6), (0, 5), (2, 5), (0, 2), (0, 3)),
+        ((0, 0), (0, 1), (0, 7), (2, 0), (3, 0), (1, 0), (1, 1), (3, 1)),
+        ((1, 7), (3, 7), (2, 7), (1, 5), (0, 6), (2, 1), (1, 2), (3, 5), (3, 4), (1, 6), (3, 6), (2, 6), (0, 5), (2, 5), (0, 2), (0, 3)),
         ((2, 2), (3, 2), (2, 3), (2, 4), (1, 3), (3, 3), (0, 4), (1, 4)),
     ),
 )

time: 82.7 us -> 83.2 us (level)
  no operation moved by 1% of the time
where the time goes in v6:
time: 83.2 us; the launch traced here: 83 us
  Pallas kernels  81.8 us (98%)
  between operations  1.29 us (2%)
    pallas_call x1, Pallas kernels, local(): pl.pallas_call(kernel, out_shape=jax.ShapeDtypeStruct((24, 128), f32), in...  80.4 us

profile of v6, /device:TPU:1, one launch (start us, length us, event | category | flops | bytes accessed | tf_op | source)
XLA Modules:
  0.0 83.0 jit_solution(11888425783778860378)
XLA Ops:
  1.3 80.4 %value_iteration.1.out = f32[24,128]{1,0:T(8,128)} custom-call(f32[256,4096]{1,0:T(8,128)} %bitcast.2, f32[256,128]{1,0:T(8,128)} %bitcast.3, s32[16]{0:T(128)} %counts_in.1, f32[16,128]{1,0:T(8,128)} %start_in.1, s32[1]{0:T(128)S(6)} %copy.8.ref_in), custom_call_target="tpu_custom_call" | custom-call | tf_op jit(solution)/shard_map/value_iteration/pallas_call | solution.py:465
  81.7 1.3 %deal.1 = (f32[16,128]{1,0:T(8,128)}, f32[4,128]{1,0:T(4,128)}, f32[4,128]{1,0:T(4,128)}) custom-call(f32[24,128]{1,0:T(8,128)} %value_iteration.1.out), custom_call_target="tpu_custom_call" | custom-call | tf_op jit(solution)/shard_map/deal/pallas_call | solution.py:512
